TPU v7x, 128 devices: a whole 4x4x4 slice. The times are simulated.
128 devices in a mesh: section: 2 (over x_hi), gx: 16 (over z, y), gy: 4 (over x_lo, core).
Axes of the slice: x: 4 (x_hi: 2, x_lo: 2; x = x_hi * 2 + x_lo), y: 4, z: 4, core: 2. Of those that a mesh axis runs over, the one named last changes fastest.
Arguments:
- inputs: bfloat16 [4, 32, 8192], P(None, None, 'gx'), may hold values from -6 to 6
- gains: bfloat16 [2, 8192], P('section', 'gx'), may hold values from 0.5 to 1.5
- query_weight: bfloat16 [2, 8192, 16384], P('section', 'gx', 'gy'), may hold values from -0.0625 to 0.0625
- key_value_weight: bfloat16 [2, 8192, 2048], P('section', 'gx', 'gy'), may hold values from -0.0625 to 0.0625
- output_weight: bfloat16 [2, 16384, 8192], P('section', 'gy', 'gx'), may hold values from -0.375 to 0.375
- rotated_key_cache: bfloat16 [2, 4, 32, 8, 1024, 128], P('section', None, 'gx', 'gy'), may hold values from -600 to 600
- stored_value_cache: bfloat16 [2, 4, 32, 8, 1024, 128], P('section', None, 'gx', 'gy'), may hold values from -6 to 6
- lengths: int32 [4, 32], P(None, 'gx'), may hold values from 2 to 1024
Outputs:
- states: bfloat16 [2, 4, 32, 8192], P('section', None, None, ('gx', 'gy'))
Inputs may be any that keep to these rules, and one draw needn't show every extreme that they name: The new token sits at position lengths; slots 0 to lengths - 1 are live.
All inputs are finite; a program needn't handle non-finite values.
Results may differ from a plain program's by a relative error of at most 0.015.
The roundings to bfloat16 on the way count: a program that leaves them out, or rounds other values in their place, can miss the bound.
Values may be sent and summed in bfloat16 or wider, within the bound.
A program may use at most 64 MiB of HBM per device.

v0:
```python
import math

import jax
import jax.numpy as jnp
from jax import lax
from jax.sharding import PartitionSpec as P

MODEL_WIDTH = 8192


ROPE_THETA = 500000.0
NORM_EPS = 1e-05


def passed_along(block, axis, distance):
    devices = range(lax.axis_size(axis))
    route = [(i - distance, i) for i in devices if i - distance in devices]
    return lax.ppermute(block, axis, route)


def in_blocks(value, dim, peers):
    before, after = (value.shape[:dim], value.shape[dim + 1 :])
    return jnp.moveaxis(value.reshape(*before, peers, -1, *after), dim, 0)


def sent_and_summed(value, axis, dim):
    tiles = in_blocks(value, dim, lax.axis_size(axis))
    arrived = lax.all_to_all(tiles, axis, split_axis=0, concat_axis=0, tiled=True)
    return arrived.sum(axis=0)


def in_one_piece(arrays, axis, dim, along):
    widths = [math.prod(a.shape[along:]) for a in arrays]
    both = jnp.concatenate(
        [a.reshape(*a.shape[:along], w) for a, w in zip(arrays, widths)], axis=along
    )
    whole = sent_and_summed(both, axis, dim)
    tiles = jnp.split(whole, [sum(widths[:k]) for k in range(1, len(widths))], axis=along)
    return tuple((b.reshape(*whole.shape[:along], *a.shape[along:]) for a, b in zip(arrays, tiles)))


def joined_along(tiles, dim):
    tiles = jnp.moveaxis(tiles, 0, dim)
    shape = tiles.shape
    return tiles.reshape(*shape[:dim], shape[dim] * shape[dim + 1], *shape[dim + 2 :])


def copy_for_each(value, axis):
    copies = jnp.broadcast_to(value, (lax.axis_size(axis), *value.shape))
    return lax.all_to_all(copies, axis, split_axis=0, concat_axis=0, tiled=True)


def collect(value, axis, dim):
    return joined_along(copy_for_each(value, axis), dim)


def taken_together(value, axis):
    everything = copy_for_each(value, axis)
    return jnp.sum(everything, axis=0)


def rotate(vectors, positions):
    half_dim = vectors.shape[-1] // 2
    frequency = ROPE_THETA ** (-2.0 * jnp.arange(half_dim, dtype=jnp.float32) / vectors.shape[-1])
    angles = positions.astype(jnp.float32)[:, None] * frequency[None, :]
    cos_part = jnp.cos(angles)[:, None, :]
    sine_part = jnp.sin(angles)[:, None, :]
    front_half = vectors[..., :half_dim]
    back_half = vectors[..., half_dim:]
    return jnp.concatenate(
        [
            front_half * cos_part - back_half * sine_part,
            back_half * cos_part + front_half * sine_part,
        ],
        axis=-1,
    )


def body(
    inputs,
    gains,
    query_weight,
    key_value_weight,
    output_weight,
    rotated_key_cache,
    stored_value_cache,
    lengths,
):
    section_id = lax.axis_index("section")
    section_count = lax.axis_size("section")
    gy_count = lax.axis_size("gy")
    gy_id = lax.axis_index("gy")
    micro_count = inputs.shape[0]
    batch_rows = inputs.shape[1]
    width_cols = inputs.shape[2]
    share_cols = width_cols // gy_count
    own_rows = lengths.shape[1]
    head_dim = rotated_key_cache.shape[5]
    kv_local = rotated_key_cache.shape[3]
    q_cols = query_weight.shape[2]
    q_local = q_cols // head_dim
    group_width = q_local // kv_local
    inv_scale = 1.0 / head_dim**0.5
    gain_row = gains[0].astype(jnp.float32)
    w_query = query_weight[0]
    w_pairs = key_value_weight[0]
    w_out = output_weight[0]
    layer_keys = rotated_key_cache[0]
    layer_values = stored_value_cache[0]
    is_first = section_id == 0
    group_count = micro_count // micro_count
    block_rows = batch_rows * micro_count
    mine_rows = own_rows * micro_count
    states = jnp.zeros((micro_count, batch_rows, share_cols), jnp.bfloat16)
    carried = jnp.zeros((block_rows, width_cols), jnp.bfloat16)
    for moment in range(group_count + section_count - 1):
        group_now = moment - section_id
        is_valid = (group_now >= 0) & (group_now < group_count)
        fresh_input = jnp.transpose(inputs, (1, 0, 2)).reshape(block_rows, width_cols)
        arrived = passed_along(carried, "section", 1) if moment > 0 else carried
        current = jnp.where(is_first, fresh_input, arrived)
        widened = current.astype(jnp.float32)
        part_squares = jnp.sum(widened * widened, axis=1)
        scaled = (widened * gain_row).astype(jnp.bfloat16)
        summed, squares = in_one_piece(
            (
                jnp.concatenate(
                    [
                        jnp.dot(scaled, w_query, preferred_element_type=jnp.float32),
                        jnp.dot(scaled, w_pairs, preferred_element_type=jnp.float32),
                    ],
                    axis=1,
                ),
                part_squares,
            ),
            "gx",
            0,
            1,
        )
        factor = lax.rsqrt(squares / MODEL_WIDTH + NORM_EPS)
        summed = factor[:, None] * summed
        lens_now = jnp.transpose(lengths, (1, 0)).reshape(mine_rows)
        query_rows = rotate(
            summed[:, :q_cols].reshape(mine_rows, q_local, head_dim), lens_now
        ).astype(jnp.bfloat16)
        query_rows = query_rows.reshape(own_rows, micro_count, kv_local, group_width, head_dim)
        key_value_pairs = summed[:, q_cols:].reshape(mine_rows, kv_local, 2, head_dim)
        fresh_key = (
            rotate(key_value_pairs[:, :, 0], lens_now)
            .astype(jnp.bfloat16)
            .reshape(own_rows, micro_count, kv_local, head_dim)
        )
        fresh_value = (
            key_value_pairs[:, :, 1]
            .astype(jnp.bfloat16)
            .reshape(own_rows, micro_count, kv_local, head_dim)
        )
        scores = (
            jnp.einsum(
                "rmhgd,mrhtd->rmhgt", query_rows, layer_keys, preferred_element_type=jnp.float32
            )
            * inv_scale
        )
        self_score = (
            jnp.einsum(
                "rmhgd,rmhd->rmhg", query_rows, fresh_key, preferred_element_type=jnp.float32
            )
            * inv_scale
        )
        lens_grid = lens_now.reshape(own_rows, micro_count)
        live_mask = (
            jnp.arange(layer_keys.shape[3], dtype=jnp.int32)[None, None, None, None, :]
            < lens_grid[:, :, None, None, None]
        )
        scores = jnp.where(live_mask, scores, -jnp.inf)
        row_top = jnp.maximum(jnp.max(scores, axis=-1), self_score)
        weights = jnp.exp(scores - row_top[..., None])
        own_weight = jnp.exp(self_score - row_top)
        denom_sum = jnp.sum(weights, axis=-1) + own_weight
        weights = (weights / denom_sum[..., None]).astype(jnp.bfloat16)
        own_weight = (own_weight / denom_sum).astype(jnp.bfloat16)
        mixed_vals = jnp.einsum(
            "rmhgt,mrhtd->rmhgd", weights, layer_values, preferred_element_type=jnp.float32
        )
        mixed_vals = (
            mixed_vals
            + own_weight.astype(jnp.float32)[..., None]
            * fresh_value.astype(jnp.float32)[:, :, :, None, :]
        )
        head_out = mixed_vals.reshape(mine_rows, q_cols).astype(jnp.bfloat16)
        partial_value = jnp.dot(
            collect(head_out, "gx", 0), w_out, preferred_element_type=jnp.float32
        )
        branch = taken_together(partial_value, "gy")
        result = (widened + branch).astype(jnp.bfloat16)
        carried = result
        share_out = lax.dynamic_slice_in_dim(result, gy_id * share_cols, share_cols, 1)
        share_block = jnp.transpose(
            share_out.reshape(batch_rows, micro_count, share_cols), (1, 0, 2)
        )
        previous = states
        updated = jnp.where(is_valid, share_block, previous)
        states = updated
    return states[None]


def solution(mesh):
    in_specs = (
        P(None, None, "gx"),
        P("section", "gx"),
        P("section", "gx", "gy"),
        P("section", "gx", "gy"),
        P("section", "gy", "gx"),
        P("section", None, "gx", "gy", None, None),
        P("section", None, "gx", "gy", None, None),
        P(None, "gx"),
    )
    out_specs = P("section", None, None, ("gx", "gy"))
    return jax.shard_map(body, mesh=mesh, in_specs=in_specs, out_specs=out_specs, check_vma=False)
```

profile of v0, /device:TPU:5, one launch (start us, length us, event | category | flops | bytes accessed | tf_op | source)
XLA Modules:
  0.0 192.4 jit_solution(6570843051090237202)
XLA Ops:
  0.0 0.0 copy-start
  0.0 0.7 mul.289
  0.7 1.0 fusion.52
  1.8 0.1 copy.89
  1.9 2.9 %fusion.6 = f32[16,8,4096]{2,1,0:T(8,128)S(1)} fusion(bf16[16,8,512]{2,1,0:T(8,128)(2,1)S(1)} %dot_general.40, bf16[1,512,4096]{2,1,0:T(8,128)(2,1)} %param.10), kind=kOutput, calls=%fused_computation.6 | convolution fusion | flops 536870912 | bytes 6422528 | tf_op jit(solution)/shard_map/dot_general | solution.py:129
  4.8 0.0 copy-done
  4.9 0.2 fusion.46
  5.1 0.1 copy.90
  5.2 0.1 concatenate.64
  5.3 1.6 pad_maximum_fusion
  6.9 7.8 %all-to-all-start = ((f32[16,8,4609]{2,1,0:T(8,128)}), f32[16,8,4609]{2,1,0:T(8,128)S(1)}, u32[]{:S(2)}, u32[]{:S(2)}) async-start(f32[16,8,4609]{2,1,0:T(8,128)} %pad_maximum_fusion), calls=%async_computation | async-start | bytes 4849664 | tf_op jit(solution)/shard_map/all_to_all | solution.py:28
  14.7 0.1 convert_element_type.116
  14.8 0.1 iota_compare_fusion
  14.9 0.1 multiply_cosine_fusion
  15.0 35.9 %all-to-all-done = f32[16,8,4609]{2,1,0:T(8,128)S(1)} async-done(((f32[16,8,4609]{2,1,0:T(8,128)}), f32[16,8,4609]{2,1,0:T(8,128)S(1)}, u32[]{:S(2)}, u32[]{:S(2)}) %all-to-all-start) | async-done | bytes 2359840 | tf_op jit(solution)/shard_map/all_to_all | solution.py:28
  50.8 0.1 reduce_sum.73
  51.0 0.0 copy-start.3
  51.0 0.1 fusion.70
  51.1 0.1 slice_multiply_fusion.1
  51.2 0.1 fusion.81
  51.3 0.1 subtract_convert_fusion.3
  51.4 0.1 maximum_bitcast_fusion
  51.5 0.1 subtract_convert_fusion.1
  51.6 0.2 fusion.60
  51.8 3.9 %fusion.82 = (f32[2,4,2,16]{3,2,1,0:T(2,128)S(1)}, f32[2,4,2,16,1024]{4,3,2,1,0:T(8,128)S(1)}) fusion(bf16[2,4,2,16,64]{4,3,2,1,0:T(8,128)(2,1)S(1)} %bitcast.100, bf16[2,4,2,16,64]{4,3,2,1,0:T(8,128)(2,1)S(1)} %bitcast.98, pred[2,4,1024]{2,1,0:T(4,128)(4,1)S(1)} %iota_compare_fusion, bf16[1,4,2,2,1024,128]{5,4,3,2,1,0:T(8,128)(2,1)} %param.13), kind=kOutput, calls=%fused_computation.111 | convolution fusion | flops 68026112 | bytes 5317632 | tf_op jit(solution)/shard_map/rmhgd,mrhtd->rmhgt/dot_general | solution.py:159
  55.7 0.3 fusion.42
  56.1 0.0 copy-done.3
  56.1 0.8 fusion.37
  56.9 0.1 broadcast_in_dim.36
  57.0 18.3 %all_to_all.30 = bf16[16,8,4096]{2,1,0:T(8,128)(2,1)S(1)} all-to-all(bf16[16,8,4096]{2,1,0:T(8,128)(2,1)S(1)} %broadcast_in_dim.36), channel_id=1, replica_groups=mesh['section'=2,'gx'=16,'gy'=4] {'gx'}, dimensions={0} | all-to-all | bytes 2097152 | tf_op jit(solution)/shard_map/all_to_all | solution.py:50
  75.3 3.0 %fusion.2 = f32[128,512]{1,0:T(8,128)S(1)} fusion(bf16[1,4096,512]{2,1,0:T(8,128)(2,1)} %param.12, bf16[16,8,4096]{2,1,0:T(8,128)(2,1)S(1)} %all_to_all.30), kind=kOutput, calls=%fused_computation.2 | convolution fusion | flops 536870912 | bytes 5505024 | tf_op jit(solution)/shard_map/dot_general | solution.py:191
  78.3 1.1 broadcast_in_dim.37
  79.4 6.4 %all-to-all-start.2 = ((f32[4,128,512]{2,1,0:T(8,128)}), f32[4,128,512]{2,1,0:T(8,128)S(1)}, u32[]{:S(2)}, u32[]{:S(2)}) async-start(f32[4,128,512]{2,1,0:T(8,128)} %broadcast_in_dim.37), calls=%async_computation.2 | async-start | bytes 2097152 | tf_op jit(solution)/shard_map/all_to_all | solution.py:50
  85.8 0.1 copy.88
  86.0 13.3 %all-to-all-done.2 = f32[4,128,512]{2,1,0:T(8,128)S(1)} async-done(((f32[4,128,512]{2,1,0:T(8,128)}), f32[4,128,512]{2,1,0:T(8,128)S(1)}, u32[]{:S(2)}, u32[]{:S(2)}) %all-to-all-start.2) | async-done | bytes 1048608 | tf_op jit(solution)/shard_map/all_to_all | solution.py:50
  99.3 0.1 reduce_sum.75
  99.4 1.3 collective-permute-start
  100.7 5.9 %collective-permute-done = bf16[128,512]{1,0:T(8,128)(2,1)S(1)} collective-permute-done((bf16[128,512]{1,0:T(8,128)(2,1)S(1)}, bf16[128,512]{1,0:T(8,128)(2,1)S(1)}, u32[]{:S(2)}, u32[]{:S(2)}) %collective-permute-start) | collective-permute-done | bytes 131104 | tf_op jit(solution)/shard_map/ppermute | solution.py:18
  106.7 2.9 %fusion.4 = f32[16,8,4096]{2,1,0:T(8,128)S(1)} fusion(bf16[1,512,4096]{2,1,0:T(8,128)(2,1)} %param.10, f32[512]{0:T(512)S(1)} %bitcast.103, bf16[128,512]{1,0:T(8,128)(2,1)S(1)} %get-tuple-element.6), kind=kOutput, calls=%fused_computation.4 | convolution fusion | flops 537067520 | bytes 6424576 | tf_op jit(solution)/shard_map/dot_general | solution.py:129
  109.6 0.2 fusion.44
  109.8 0.1 multiply_reduce_fusion
  109.9 0.2 concatenate.65
  110.1 0.2 pad_maximum_fusion.1
  110.3 33.1 %all_to_all.31 = f32[16,8,4609]{2,1,0:T(8,128)S(1)} all-to-all(f32[16,8,4609]{2,1,0:T(8,128)S(1)} %pad_maximum_fusion.1), channel_id=1, replica_groups=mesh['section'=2,'gx'=16,'gy'=4] {'gx'}, dimensions={0} | all-to-all | bytes 4719616 | tf_op jit(solution)/shard_map/all_to_all | solution.py:28
  143.5 0.1 reduce_sum.77
  143.6 0.0 copy-start.4
  143.6 0.1 fusion.67
  143.7 0.1 slice_multiply_fusion
  143.9 0.1 subtract_convert_fusion.2
  143.9 0.1 fusion.80
  144.0 0.1 maximum_bitcast_fusion.1
  144.1 0.1 subtract_convert_fusion
  144.2 3.8 %fusion.83 = (f32[2,4,2,16]{3,2,1,0:T(2,128)S(1)}, f32[2,4,2,16,1024]{4,3,2,1,0:T(8,128)S(1)}) fusion(bf16[2,4,2,16,64]{4,3,2,1,0:T(8,128)(2,1)S(1)} %bitcast.95, bf16[2,4,2,16,64]{4,3,2,1,0:T(8,128)(2,1)S(1)} %bitcast.93, pred[2,4,1024]{2,1,0:T(4,128)(4,1)S(1)} %iota_compare_fusion, bf16[1,4,2,2,1024,128]{5,4,3,2,1,0:T(8,128)(2,1)} %param.13), kind=kOutput, calls=%fused_computation.112 | convolution fusion | flops 68026112 | bytes 5317632 | tf_op jit(solution)/shard_map/rmhgd,mrhtd->rmhgt/dot_general | solution.py:159
  148.0 0.2 fusion.59
  148.2 0.3 fusion.43
  148.6 0.8 fusion.34
  149.4 0.1 broadcast_in_dim.38
  149.5 16.3 %all_to_all.32 = bf16[16,8,4096]{2,1,0:T(8,128)(2,1)S(1)} all-to-all(bf16[16,8,4096]{2,1,0:T(8,128)(2,1)S(1)} %broadcast_in_dim.38), channel_id=1, replica_groups=mesh['section'=2,'gx'=16,'gy'=4] {'gx'}, dimensions={0} | all-to-all | bytes 2097152 | tf_op jit(solution)/shard_map/all_to_all | solution.py:50
  165.9 3.0 %fusion = f32[128,512]{1,0:T(8,128)S(1)} fusion(bf16[1,4096,512]{2,1,0:T(8,128)(2,1)} %param.12, bf16[16,8,4096]{2,1,0:T(8,128)(2,1)S(1)} %all_to_all.32), kind=kOutput, calls=%fused_computation | convolution fusion | flops 536870912 | bytes 5505024 | tf_op jit(solution)/shard_map/dot_general | solution.py:191
  168.8 1.1 broadcast_in_dim.39
  169.9 8.2 %all-to-all-start.5 = ((f32[4,128,512]{2,1,0:T(8,128)}), f32[4,128,512]{2,1,0:T(8,128)S(1)}, u32[]{:S(2)}, u32[]{:S(2)}) async-start(f32[4,128,512]{2,1,0:T(8,128)} %broadcast_in_dim.39), calls=%async_computation.5 | async-start | bytes 2097152 | tf_op jit(solution)/shard_map/all_to_all | solution.py:50
  178.2 13.5 %all-to-all-done.5 = f32[4,128,512]{2,1,0:T(8,128)S(1)} async-done(((f32[4,128,512]{2,1,0:T(8,128)}), f32[4,128,512]{2,1,0:T(8,128)S(1)}, u32[]{:S(2)}, u32[]{:S(2)}) %all-to-all-start.5) | async-done | bytes 1048608 | tf_op jit(solution)/shard_map/all_to_all | solution.py:50
  191.6 0.1 reduce_sum.79
  191.8 0.6 copy.104
  (28 shorter events, 0.4 us)
Async XLA Ops:
  0.0 4.8 %copy-start = (bf16[1,512,512]{2,1,0:T(8,128)(2,1)S(1)}, bf16[1,512,512]{2,1,0:T(8,128)(2,1)}, u32[]{:S(2)}) copy-start(bf16[1,512,512]{2,1,0:T(8,128)(2,1)} %param.11) | copy-start | bytes 1572868
  5.3 9.4 %copy-start.2 = (s32[4,2]{0,1:T(2,128)S(1)}, s32[4,2]{0,1:T(2,128)}, u32[]{:S(2)}) copy-start(s32[4,2]{0,1:T(2,128)} %param.15) | copy-start | bytes 100
  6.9 44.0 %all-to-all-start = ((f32[16,8,4609]{2,1,0:T(8,128)}), f32[16,8,4609]{2,1,0:T(8,128)S(1)}, u32[]{:S(2)}, u32[]{:S(2)}) async-start(f32[16,8,4609]{2,1,0:T(8,128)} %pad_maximum_fusion), calls=%async_computation | async-start | bytes 4849664 | tf_op jit(solution)/shard_map/all_to_all | solution.py:28
  51.0 5.1 %copy-start.3 = (bf16[1,4,2,2,1024,128]{5,4,3,2,1,0:T(8,128)(2,1)S(1)}, bf16[1,4,2,2,1024,128]{5,4,3,2,1,0:T(8,128)(2,1)}, u32[]{:S(2)}) copy-start(bf16[1,4,2,2,1024,128]{5,4,3,2,1,0:T(8,128)(2,1)} %param.14) | copy-start | bytes 12582916
  75.3 10.5 %copy-start.1 = (bf16[4,32,512]{2,1,0:T(8,128)(2,1)S(1)}, bf16[4,32,512]{2,1,0:T(8,128)(2,1)}, u32[]{:S(2)}) copy-start(bf16[4,32,512]{2,1,0:T(8,128)(2,1)} %param.8) | copy-start | bytes 393220
  79.4 19.9 %all-to-all-start.2 = ((f32[4,128,512]{2,1,0:T(8,128)}), f32[4,128,512]{2,1,0:T(8,128)S(1)}, u32[]{:S(2)}, u32[]{:S(2)}) async-start(f32[4,128,512]{2,1,0:T(8,128)} %broadcast_in_dim.37), calls=%async_computation.2 | async-start | bytes 2097152 | tf_op jit(solution)/shard_map/all_to_all | solution.py:50
  99.4 7.2 %collective-permute-start = (bf16[128,512]{1,0:T(8,128)(2,1)S(1)}, bf16[128,512]{1,0:T(8,128)(2,1)S(1)}, u32[]{:S(2)}, u32[]{:S(2)}) collective-permute-start(bf16[128,512]{1,0:T(8,128)(2,1)S(1)} %add_convert_fusion), channel_id=1, source_target_pairs={{0,64},{1,65},{2,66},{3,67},{4,68},{5,69},{6,70},{7,71},{8,72},{9,... | collective-permute-start | bytes 393224 | tf_op jit(solution)/shard_map/ppermute | solution.py:18
  143.6 5.0 %copy-start.4 = (bf16[1,4,2,2,1024,128]{5,4,3,2,1,0:T(8,128)(2,1)S(1)}, bf16[1,4,2,2,1024,128]{5,4,3,2,1,0:T(8,128)(2,1)}, u32[]{:S(2)}) copy-start(bf16[1,4,2,2,1024,128]{5,4,3,2,1,0:T(8,128)(2,1)} %param.14) | copy-start | bytes 12582916
  169.9 21.7 %all-to-all-start.5 = ((f32[4,128,512]{2,1,0:T(8,128)}), f32[4,128,512]{2,1,0:T(8,128)S(1)}, u32[]{:S(2)}, u32[]{:S(2)}) async-start(f32[4,128,512]{2,1,0:T(8,128)} %broadcast_in_dim.39), calls=%async_computation.5 | async-start | bytes 2097152 | tf_op jit(solution)/shard_map/all_to_all | solution.py:50
where the time goes:
time: 193 us; the launch traced here: 192 us
  waiting for transfers between devices  68.6 us (36%)
  blocking collectives  67.8 us (35%)
  starting transfers between devices  23.7 us (12%)
  matrix products  21.9 us (11%)
  other arithmetic  5.93 us (3%)
  local copies, waits for them, and re-layouts  4.13 us (2%)
    all_to_all x1, waiting for transfers between devices, sent_and_summed(): lax.all_to_all(tiles, axis, split_axis=0, concat_axis=0, tiled=True)  35.9 us
    all_to_all x2, blocking collectives, copy_for_each(): return lax.all_to_all(copies, axis, split_axis=0, concat_axis=0, tiled=True)  34.6 us
    all_to_all x1, blocking collectives, sent_and_summed(): lax.all_to_all(tiles, axis, split_axis=0, concat_axis=0, tiled=True)  33.1 us
    all_to_all x2, waiting for transfers between devices, copy_for_each(): return lax.all_to_all(copies, axis, split_axis=0, concat_axis=0, tiled=True)  26.8 us
    all_to_all x2, starting transfers between devices, copy_for_each(): return lax.all_to_all(copies, axis, split_axis=0, concat_axis=0, tiled=True)  14.6 us
    all_to_all x1, starting transfers between devices, sent_and_summed(): lax.all_to_all(tiles, axis, split_axis=0, concat_axis=0, tiled=True)  7.77 us
    dot_general x2, matrix products, body(): jnp.einsum('rmhgd,mrhtd->rmhgt', query_rows, layer_keys, preferred_elemen...  7.73 us
    dot_general x2, matrix products, body(): jnp.dot(collect(head_out, 'gx', 0), w_out, preferred_element_type=jnp.flo...  5.95 us
  transfers between devices with their start and end apart: 4, of which 4 were waited for; matrix products, arithmetic and copies ran while one was open for 0% of the time, Pallas kernels for 0%

commit v1 on v0

v1 whole, which is shorter than its diff:
```python
import functools

import jax
import jax.numpy as jnp
from jax import lax
from jax.experimental import pallas as pl
from jax.experimental.pallas import tpu as pltpu
from jax.sharding import PartitionSpec as P

MODEL_WIDTH = 8192
ROPE_THETA = 500000.0
NORM_EPS = 1e-05

MESH = pl.DeviceIdType.MESH
MICRO = 4
ROWS = 32
TILES = 19
LOW = 80
HIGH = 72
STAGES = 7


def swapped_rows(src, dst):
    for a in range(4):
        for b in range(4):
            dst[8 * b + 2 * a : 8 * b + 2 * a + 2, :] = src[8 * a + 2 * b : 8 * a + 2 * b + 2, :]


def kernel(
    x_hbm,
    gain_ref,
    rope_ref,
    len_ref,
    wq_hbm,
    wkv_hbm,
    wo_hbm,
    k_hbm,
    v_hbm,
    out_ref,
    xs,
    wq,
    wkv,
    wo,
    keys,
    values,
    wide,
    turned,
    part,
    lo2,
    lod,
    los,
    hi2,
    hid,
    his,
    whole,
    piece,
    piece_in,
    total,
    heads,
    spread,
    lhs_in,
    lhs,
    branch0,
    branch1,
    branch2,
    share,
    share_in,
    result,
    local_sem,
    s1_send,
    s1_recv,
    s2_send,
    s2_recv,
    g1_send,
    g1_recv,
    g2_send,
    g2_recv,
    gy_send,
    gy_recv,
    x_send,
    x_recv,
):
    sec = lax.axis_index("section")
    gx = lax.axis_index("gx")
    gy = lax.axis_index("gy")
    z = gx // 4
    y = gx % 4

    def along_z(k):
        return (sec, ((z + k) % 4) * 4 + y, gy)

    def along_y(k):
        return (sec, z * 4 + (y + k) % 4, gy)

    def along_gy(k):
        return (sec, gx, (gy + k) % 4)

    firsts = ((z, along_z), (y, along_y))
    seconds = ((y, along_y), (z, along_z))

    def remote(src, dst, send, recv, dev):
        return pltpu.make_async_remote_copy(
            src_ref=src, dst_ref=dst, send_sem=send, recv_sem=recv, device_id=dev, device_id_type=MESH
        )

    local = []

    def stage_in(src, dst):
        copy = pltpu.make_async_copy(src, dst, local_sem.at[len(local)])
        local.append(copy)
        return copy

    x_copies = [stage_in(x_hbm.at[:, :, pl.ds(128 * c, 128)], xs.at[:, c]) for c in range(4)]
    wq_copies = []
    wkv_copies = []
    for h in range(2):
        wq_copies.append(stage_in(wq_hbm.at[0, :, pl.ds(2048 * h, 2048)], wq.at[h]))
        wkv_copies.append(stage_in(wkv_hbm.at[0, :, pl.ds(256 * h, 256)], wkv.at[h]))
    k_copy = stage_in(k_hbm.at[0], keys)
    v_copy = stage_in(v_hbm.at[0], values)
    wo_copy = stage_in(wo_hbm.at[0], wo)

    @pl.when(sec == 0)
    def _():
        for copy in x_copies:
            copy.start()

    for h in range(2):
        wq_copies[h].start()
        wkv_copies[h].start()
    k_copy.start()
    v_copy.start()
    wo_copy.start()

    barrier = pltpu.get_barrier_semaphore()
    partners = [along_z(k) for k in (1, 2, 3)] + [along_y(k) for k in (1, 2, 3)]
    partners += [along_gy(k) for k in (1, 2, 3)]
    partners += [(1 - sec, gx, (gy + k) % 4) for k in range(4)]
    for dev in partners:
        pl.semaphore_signal(barrier, inc=1, device_id=dev, device_id_type=MESH)

    def first_copies(m, h):
        p, dev = firsts[h]
        up, down, far = (p + 1) % 4, (p + 3) % 4, (p + 2) % 4
        low, high = pl.ds(0, LOW), pl.ds(LOW, HIGH)
        src = part.at[m, h]
        ss, rs = s1_send.at[m, h], s1_recv.at[m, h]
        return (
            remote(src.at[far, low], lo2.at[m, h], ss.at[0], rs.at[0], dev(1)),
            remote(src.at[far, high], hi2.at[m, h], ss.at[1], rs.at[1], dev(3)),
            remote(src.at[up, high], hid.at[m, h], ss.at[2], rs.at[2], dev(1)),
            remote(src.at[down, low], lod.at[m, h], ss.at[3], rs.at[3], dev(3)),
        )

    def relay_copies(m, h):
        p, dev = firsts[h]
        ss, rs = s1_send.at[m, h], s1_recv.at[m, h]
        return (
            remote(lo2.at[m, h], los.at[m, h], ss.at[4], rs.at[4], dev(1)),
            remote(hi2.at[m, h], his.at[m, h], ss.at[5], rs.at[5], dev(3)),
        )

    def second_copies(m, h):
        p, dev = seconds[h]
        return [
            remote(
                piece.at[m, h, (p + k) % 4],
                piece_in.at[m, h, k - 1],
                s2_send.at[m, h, k - 1],
                s2_recv.at[m, h, k - 1],
                dev(k),
            )
            for k in (2, 1, 3)
        ]

    def gather1_copies(m, h, slot_of):
        p, dev = seconds[h]
        return [
            remote(
                heads.at[m, h, slot_of(p, k)],
                heads.at[m, h, slot_of(p, k)],
                g1_send.at[m, h, k - 1],
                g1_recv.at[m, h, k - 1],
                dev(k),
            )
            for k in (2, 1, 3)
        ]

    def gather2_copies(m, h, slot_of):
        p, dev = firsts[h]
        return [
            remote(
                lhs_in.at[m, h, slot_of(p, k)],
                lhs_in.at[m, h, slot_of(p, k)],
                g2_send.at[m, h, k - 1],
                g2_recv.at[m, h, k - 1],
                dev(k),
            )
            for k in (2, 1, 3)
        ]

    def sender_slot(p, k):
        return p

    def receiver_slot(p, k):
        return (p + 4 - k) % 4

    def gy_copies(m):
        return [
            remote(
                share.at[m, (gy + k) % 4],
                share_in.at[m, k - 1],
                gy_send.at[m, k - 1],
                gy_recv.at[m, k - 1],
                along_gy(k),
            )
            for k in (1, 2, 3)
        ]

    def x_copy_out(m, k):
        return remote(
            result.at[m], xs.at[m, gy], x_send.at[m, k], x_recv.at[m, k], (1, gx, (gy + k) % 4)
        )

    def x_copy_in(m, k):
        slot = xs.at[m, (gy + 4 - k) % 4]
        return remote(slot, slot, x_send.at[m, k], x_recv.at[m, k], (0, gx, gy))

    def project(m):
        @pl.when((m == 0) & (sec == 0))
        def _():
            for copy in x_copies:
                copy.wait()

        @pl.when(sec == 1)
        def _():
            for k in range(4):
                x_copy_in(m, k).wait_recv()

        for c in range(4):
            wide[c] = xs[m, c].astype(jnp.float32)
        for h in range(2):

            @pl.when(m == 0)
            def _(h=h):
                wq_copies[h].wait()
                wkv_copies[h].wait()

            if h == 1:
                for c in range(4):
                    swapped_rows(wide.at[c], turned.at[c])
            blocks = [(wide if h == 0 else turned)[c] for c in range(4)]
            scaled = jnp.concatenate(
                [(b * gain_ref[:, 128 * c : 128 * c + 128]).astype(jnp.bfloat16) for c, b in enumerate(blocks)],
                axis=1,
            )
            squares = sum(b * b for b in blocks[1:]) + blocks[0] * blocks[0]
            for c in range(4):
                part[m, h, c, 144:152, :] = squares[8 * c : 8 * c + 8, :]
            for col in range(5):
                width = 512 if col < 4 else 256
                weight = wq[h, :, 512 * col : 512 * col + 512] if col < 4 else wkv[h]
                sums = jnp.dot(scaled, weight, preferred_element_type=jnp.float32)
                for c in range(4):
                    for j in range(width // 128):
                        tile = 4 * col + j
                        part[m, h, c, 8 * tile : 8 * tile + 8, :] = sums[
                            8 * c : 8 * c + 8, 128 * j : 128 * j + 128
                        ]
            if h == 0:

                @pl.when(m == 0)
                def _():
                    pl.semaphore_wait(barrier, len(partners))

            for copy in first_copies(m, h):
                copy.start()

    def relay(m):
        for h in range(2):
            p, _ = firsts[h]
            a, b, _, _ = first_copies(m, h)
            a.wait_recv()
            lo2[m, h] = lo2[m, h] + part[m, h, (p + 1) % 4, 0:LOW, :]
            relay_copies(m, h)[0].start()
            b.wait_recv()
            hi2[m, h] = hi2[m, h] + part[m, h, (p + 3) % 4, LOW : LOW + HIGH, :]
            relay_copies(m, h)[1].start()

    def second(m):
        for h in range(2):
            p, _ = firsts[h]
            _, _, c, d = first_copies(m, h)
            e, f = relay_copies(m, h)
            c.wait_recv()
            d.wait_recv()
            e.wait_recv()
            whole[0:LOW, :] = part[m, h, p, 0:LOW, :] + lod[m, h] + los[m, h]
            f.wait_recv()
            whole[LOW : LOW + HIGH, :] = part[m, h, p, LOW : LOW + HIGH, :] + hid[m, h] + his[m, h]
            for q in range(4):
                for s in range(2):
                    piece[m, h, q, 16 * s : 16 * s + 16, :] = whole[pl.ds(2 * q + s, 16, stride=8), :]
                for i in range(3):
                    piece[m, h, q, 32 + 2 * i : 34 + 2 * i, :] = whole[
                        128 + 8 * i + 2 * q : 130 + 8 * i + 2 * q, :
                    ]
                piece[m, h, q, 38:40, :] = whole[144 + 2 * q : 146 + 2 * q, :]
            for copy in second_copies(m, h):
                copy.start()

    def attend(m):
        @pl.when(m == 0)
        def _():
            k_copy.wait()
            v_copy.wait()

        inv_scale = 1.0 / 128**0.5
        slot = lax.broadcasted_iota(jnp.int32, (16, 1024), 1)
        for h in range(2):
            p, _ = seconds[h]
            for copy in second_copies(m, h):
                copy.wait_recv()
            total[...] = piece[m, h, p] + piece_in[m, h, 0] + piece_in[m, h, 1] + piece_in[m, h, 2]
            for s in range(2):
                squares = jnp.sum(total[36 + s : 37 + s, :], axis=1, keepdims=True)
                factor = lax.rsqrt(squares / MODEL_WIDTH + NORM_EPS)
                cosine, sine = rope_ref[m, s, 0:1, :], rope_ref[m, s, 1:2, :]
                query = total[16 * s : 16 * s + 16, :] * factor
                query = (query * cosine + pltpu.roll(query, 64, 1) * sine).astype(jnp.bfloat16)
                fresh_key = total[32 + s : 33 + s, :] * factor
                fresh_key = fresh_key * cosine + pltpu.roll(fresh_key, 64, 1) * sine
                fresh_key = fresh_key.astype(jnp.bfloat16).astype(jnp.float32)
                fresh_value = (total[34 + s : 35 + s, :] * factor).astype(jnp.bfloat16).astype(jnp.float32)
                scores = (
                    lax.dot_general(
                        query,
                        keys[m, s, h],
                        (((1,), (1,)), ((), ())),
                        preferred_element_type=jnp.float32,
                    )
                    * inv_scale
                )
                own = jnp.sum(query.astype(jnp.float32) * fresh_key, axis=1, keepdims=True) * inv_scale
                scores = jnp.where(slot < len_ref[m, s], scores, -jnp.inf)
                top = jnp.maximum(jnp.max(scores, axis=1, keepdims=True), own)
                weights = jnp.exp(scores - top)
                own = jnp.exp(own - top)
                scale = 1.0 / (jnp.sum(weights, axis=1, keepdims=True) + own)
                weights = (weights * scale).astype(jnp.bfloat16)
                own = (own * scale).astype(jnp.bfloat16).astype(jnp.float32)
                mixed = jnp.dot(weights, values[m, s, h], preferred_element_type=jnp.float32)
                mixed = mixed + own * fresh_value
                heads[m, h, p, 16 * s : 16 * s + 16, :] = mixed.astype(jnp.bfloat16)
            for copy in gather1_copies(m, h, sender_slot):
                copy.start()

    def regroup(m):
        for h in range(2):
            p, _ = firsts[h]
            for copy in gather1_copies(m, h, receiver_slot):
                copy.wait_recv()
            for b in range(4):
                spread[32 * b : 32 * b + 32, :] = heads[m, h, b].astype(jnp.float32)
            for j in range(16):
                lhs_in[m, h, p, j] = spread[pl.ds(j, 8, stride=16), :].astype(jnp.bfloat16)
            for copy in gather2_copies(m, h, sender_slot):
                copy.start()

    def output(m):
        @pl.when(m == 0)
        def _():
            wo_copy.wait()

        for h in range(2):
            for copy in gather2_copies(m, h, receiver_slot):
                copy.wait_recv()
            for j in range(16):
                rows = [lhs_in[m, h, b, j].astype(jnp.float32) for b in range(4)]
                lhs[:, 128 * j : 128 * j + 128] = jnp.concatenate(rows, axis=0).astype(jnp.bfloat16)
            sums = jnp.dot(
                lhs[...], wo[2048 * h : 2048 * h + 2048, :], preferred_element_type=jnp.float32
            )
            if h == 0:
                branch0[...] = sums
            else:
                branch1[...] = sums
        swapped_rows(branch1, branch2)
        for c in range(4):
            cols = slice(128 * c, 128 * c + 128)
            share[m, c] = branch0[:, cols] + branch2[:, cols]
        for copy in gy_copies(m):
            copy.start()

    def finish(m):
        for copy in gy_copies(m):
            copy.wait_recv()
        branch = share[m, gy] + share_in[m, 0] + share_in[m, 1] + share_in[m, 2]
        state = (xs[m, gy].astype(jnp.float32) + branch).astype(jnp.bfloat16)
        out_ref[m] = state

        @pl.when(sec == 0)
        def _():
            result[m] = state
            for k in range(4):
                x_copy_out(m, k).start()

    def moment(t, carry):
        for n, stage in enumerate((project, relay, second, attend, regroup, output, finish)):
            m = t - n

            @pl.when((m >= 0) & (m < MICRO))
            def _(stage=stage, m=m):
                stage(m)

        return carry

    lax.fori_loop(0, MICRO + STAGES - 1, moment, 0)

    def settle(m, carry):
        for h in range(2):
            for copy in (
                *first_copies(m, h),
                *relay_copies(m, h),
                *second_copies(m, h),
                *gather1_copies(m, h, sender_slot),
                *gather2_copies(m, h, sender_slot),
            ):
                copy.wait_send()
        for copy in gy_copies(m):
            copy.wait_send()

        @pl.when(sec == 0)
        def _():
            for k in range(4):
                x_copy_out(m, k).wait_send()

        return carry

    lax.fori_loop(0, MICRO, settle, 0)


def body(inputs, gains, query_weight, key_value_weight, output_weight, key_cache, value_cache, lengths):
    half = 64
    frequency = ROPE_THETA ** (-2.0 * jnp.arange(half, dtype=jnp.float32) / 128)
    angles = lengths.astype(jnp.float32)[:, :, None] * frequency
    cosine, sine = jnp.cos(angles), jnp.sin(angles)
    rope = jnp.stack(
        [jnp.concatenate([cosine, cosine], axis=-1), jnp.concatenate([-sine, sine], axis=-1)], axis=2
    )
    f32, bf16 = jnp.float32, jnp.bfloat16
    vmem, anywhere = pl.BlockSpec(memory_space=pltpu.VMEM), pl.BlockSpec(memory_space=pl.ANY)
    dma = pltpu.SemaphoreType.DMA
    low, high = pltpu.VMEM((4, 2, LOW, 128), f32), pltpu.VMEM((4, 2, HIGH, 128), f32)
    states = pl.pallas_call(
        kernel,
        out_shape=jax.ShapeDtypeStruct((MICRO, ROWS, 128), bf16),
        in_specs=[anywhere, vmem, vmem, pl.BlockSpec(memory_space=pltpu.SMEM)] + [anywhere] * 5,
        out_specs=vmem,
        scratch_shapes=[
            pltpu.VMEM((4, 4, ROWS, 128), bf16),
            pltpu.VMEM((2, 512, 2048), bf16),
            pltpu.VMEM((2, 512, 256), bf16),
            pltpu.VMEM((4096, 512), bf16),
            pltpu.VMEM((4, 2, 2, 1024, 128), bf16),
            pltpu.VMEM((4, 2, 2, 1024, 128), bf16),
            pltpu.VMEM((4, ROWS, 128), f32),
            pltpu.VMEM((4, ROWS, 128), f32),
            pltpu.VMEM((4, 2, 4, 8 * TILES, 128), f32),
            low,
            low,
            low,
            high,
            high,
            high,
            pltpu.VMEM((8 * TILES, 128), f32),
            pltpu.VMEM((4, 2, 4, 40, 128), f32),
            pltpu.VMEM((4, 2, 3, 40, 128), f32),
            pltpu.VMEM((40, 128), f32),
            pltpu.VMEM((4, 2, 4, 32, 128), bf16),
            pltpu.VMEM((128, 128), f32),
            pltpu.VMEM((4, 2, 4, 16, 8, 128), bf16),
            pltpu.VMEM((ROWS, 2048), bf16),
            pltpu.VMEM((ROWS, 512), f32),
            pltpu.VMEM((ROWS, 512), f32),
            pltpu.VMEM((ROWS, 512), f32),
            pltpu.VMEM((4, 4, ROWS, 128), f32),
            pltpu.VMEM((4, 3, ROWS, 128), f32),
            pltpu.VMEM((4, ROWS, 128), bf16),
            dma((11,)),
            dma((4, 2, 6)),
            dma((4, 2, 6)),
            dma((4, 2, 3)),
            dma((4, 2, 3)),
            dma((4, 2, 3)),
            dma((4, 2, 3)),
            dma((4, 2, 3)),
            dma((4, 2, 3)),
            dma((4, 3)),
            dma((4, 3)),
            dma((4, 4)),
            dma((4, 4)),
        ],
        compiler_params=pltpu.CompilerParams(
            collective_id=0, has_side_effects=True, vmem_limit_bytes=56 * 1024 * 1024
        ),
        name="relay_layers",
    )(
        inputs,
        gains.astype(f32),
        rope,
        lengths,
        query_weight,
        key_value_weight,
        output_weight,
        key_cache,
        value_cache,
    )
    return states[None]


def solution(mesh):
    in_specs = (
        P(None, None, "gx"),
        P("section", "gx"),
        P("section", "gx", "gy"),
        P("section", "gx", "gy"),
        P("section", "gy", "gx"),
        P("section", None, "gx", "gy", None, None),
        P("section", None, "gx", "gy", None, None),
        P(None, "gx"),
    )
    out_specs = P("section", None, None, ("gx", "gy"))
    return jax.shard_map(body, mesh=mesh, in_specs=in_specs, out_specs=out_specs, check_vma=False)
```

time: 193 us -> 83.9 us (0.43)
  Pallas kernels: 0 us -> 78 us
  waiting for transfers between devices: 68.6 us -> 0 us
  blocking collectives: 67.8 us -> 0 us
  starting transfers between devices: 23.7 us -> 0 us
  matrix products: 21.9 us -> 0 us
  other arithmetic: 5.93 us -> 2.78 us
    pallas_call x0 -> x1, Pallas kernels: none -> 78 us  [body(): pl.pallas_call(kernel, out_shape=jax.ShapeDtypeStruct((MICRO, ROWS, 128),...]
    all_to_all x3 -> x0, blocking collectives: 67.8 us -> none  [the longest x2 34.6 us: copy_for_each(): return lax.all_to_all(copies, axis, split_axis=0, concat_axis=0, tiled=True)]
    all_to_all x3 -> x0, waiting for transfers between devices: 62.7 us -> none  [the longest x1 35.9 us: sent_and_summed(): lax.all_to_all(tiles, axis, split_axis=0, concat_axis=0, tiled=True)]
    all_to_all x3 -> x0, starting transfers between devices: 22.4 us -> none  [the longest x2 14.6 us: copy_for_each(): return lax.all_to_all(copies, axis, split_axis=0, concat_axis=0, tiled=True)]
    dot_general x12 -> x0, matrix products: 21.9 us -> none  [the longest x2 7.73 us: body(): jnp.einsum('rmhgd,mrhtd->rmhgt', query_rows, layer_keys, preferred_elemen...]
    ppermute x1 -> x0, waiting for transfers between devices: 5.92 us -> none  [passed_along(): return lax.ppermute(block, axis, route)]
    broadcast_in_dim x5 -> x0, local copies, waits for them, and re-layouts: 3.05 us -> none  [the longest x4 2.43 us: copy_for_each(): copies = jnp.broadcast_to(value, (lax.axis_size(axis), *value.shape))]
    unnamed x10 -> x2, local copies, waits for them, and re-layouts: 0.02 us -> 2.71 us
  transfers between devices with their start and end apart: 4 -> 0, of which waited for: 4 -> 0; matrix products, arithmetic and copies ran while one was open for 0% -> 0% of each run, Pallas kernels for 0% -> 0%
where the time goes in v1:
time: 83.9 us; the launch traced here: 83.6 us
  Pallas kernels  78 us (93%)
  local copies, waits for them, and re-layouts  2.8 us (3%)
  other arithmetic  2.78 us (3%)
    pallas_call x1, Pallas kernels, body(): pl.pallas_call(kernel, out_shape=jax.ShapeDtypeStruct((MICRO, ROWS, 128),...  78 us
    unnamed x2, local copies, waits for them, and re-layouts  2.71 us

profile of v1, /device:TPU:5, one launch (start us, length us, event | category | flops | bytes accessed | tf_op | source)
XLA Modules:
  0.0 83.6 jit_solution(18067458283564242842)
XLA Ops:
  0.0 0.7 convert_element_type.7
  0.7 0.1 copy.9
  0.8 1.2 %convert_element_type.6.gain_ref = f32[1,512]{1,0:T(1,128)} convert(bf16[1,512]{1,0:T(2,128)(2,1)} %param.9) | non-fusion elementwise | flops 512 | bytes 3072 | tf_op jit(solution)/shard_map/convert_element_type | solution.py:510
  2.0 1.3 %copy.11.len_ref = s32[4,2]{1,0:T(4,128)} copy(s32[4,2]{0,1:T(2,128)} %param.15) | data formatting | bytes 64 | tf_op args[7]
  3.4 0.1 multiply_cosine_fusion
  3.5 0.1 pad_maximum_fusion.1
  3.6 0.6 pad_maximum_fusion.rope_ref
  4.2 78.0 %relay_layers.1 = bf16[4,32,128]{2,1,0:T(8,128)(2,1)} custom-call(bf16[4,32,512]{2,1,0:T(8,128)(2,1)} %x_hbm.1, f32[1,512]{1,0:T(1,128)} %convert_element_type.6.gain_ref, f32[4,2,2,128]{3,2,1,0:T(2,128)} %pad_maximum_fusion.rope_ref, s32[4,2]{1,0:T(4,128)} %copy.11.len_ref, bf16[1,512,4096]{2,1,0:T(8,128)(2,1)} %wq_hbm.1, bf16[1,512,512]{2,1,0:T(8,128)(2,1)} %wkv_hbm.1, ...), custom_call_target="tpu_custom_call" | custom-call | tf_op jit(solution)/shard_map/relay_layers/pallas_call | solution.py:455
  82.2 1.4 %copy.13 = bf16[1,4,32,128]{3,2,1,0:T(8,128)(2,1)} copy(bf16[1,4,32,128]{3,2,1,0:T(8,128)(2,1)} %bitcast.5) | data formatting | bytes 65536
  (1 shorter events, 0.0 us)

commit v2 on v1

--- a/solution.py
+++ b/solution.py
@@ -1,7 +1,6 @@
-import functools
-
 import jax
 import jax.numpy as jnp
+import numpy as np
 from jax import lax
 from jax.experimental import pallas as pl
 from jax.experimental.pallas import tpu as pltpu
@@ -18,6 +17,7 @@
 LOW = 80
 HIGH = 72
 STAGES = 7
+SENT_ROWS = 1728
 
 
 def swapped_rows(src, dst):
@@ -28,15 +28,21 @@
 
 def kernel(
     x_hbm,
-    gain_ref,
-    rope_ref,
-    len_ref,
+    gain_hbm,
+    freq_hbm,
+    len_hbm,
     wq_hbm,
     wkv_hbm,
     wo_hbm,
     k_hbm,
     v_hbm,
-    out_ref,
+    out_hbm,
+    gain_in,
+    freq_in,
+    len_ref,
+    gain_ref,
+    rope_ref,
+    sent,
     xs,
     wq,
     wkv,
@@ -67,15 +73,12 @@
     share_in,
     result,
     local_sem,
-    s1_send,
+    send_sem,
+    out_sem,
     s1_recv,
-    s2_send,
     s2_recv,
-    g1_send,
     g1_recv,
-    g2_send,
     g2_recv,
-    gy_send,
     gy_recv,
     x_send,
     x_recv,
@@ -110,6 +113,7 @@
         local.append(copy)
         return copy
 
+    small = [stage_in(gain_hbm, gain_in), stage_in(freq_hbm, freq_in), stage_in(len_hbm, len_ref)]
     x_copies = [stage_in(x_hbm.at[:, :, pl.ds(128 * c, 128)], xs.at[:, c]) for c in range(4)]
     wq_copies = []
     wkv_copies = []
@@ -120,6 +124,9 @@
     v_copy = stage_in(v_hbm.at[0], values)
     wo_copy = stage_in(wo_hbm.at[0], wo)
 
+    for copy in small:
+        copy.start()
+
     @pl.when(sec == 0)
     def _():
         for copy in x_copies:
@@ -139,25 +146,39 @@
     for dev in partners:
         pl.semaphore_signal(barrier, inc=1, device_id=dev, device_id_type=MESH)
 
+    for copy in small:
+        copy.wait()
+    gain_ref[...] = gain_in[...].astype(jnp.float32)
+    row = lax.broadcasted_iota(jnp.int32, (8, 128), 0)
+    lane = lax.broadcasted_iota(jnp.int32, (8, 128), 1)
+    spots = jnp.zeros((8, 128), jnp.int32)
+    for m in range(MICRO):
+        for i in range(2):
+            spots = jnp.where(row == 2 * m + i, len_ref[i, m], spots)
+    angles = spots.astype(jnp.float32) * freq_in[...]
+    sine = jnp.sin(angles)
+    rope_ref[0] = jnp.cos(angles)
+    rope_ref[1] = jnp.where(lane < 64, -sine, sine)
+
     def first_copies(m, h):
         p, dev = firsts[h]
         up, down, far = (p + 1) % 4, (p + 3) % 4, (p + 2) % 4
         low, high = pl.ds(0, LOW), pl.ds(LOW, HIGH)
         src = part.at[m, h]
-        ss, rs = s1_send.at[m, h], s1_recv.at[m, h]
+        ss, rs = send_sem.at[m], s1_recv.at[m, h]
         return (
-            remote(src.at[far, low], lo2.at[m, h], ss.at[0], rs.at[0], dev(1)),
-            remote(src.at[far, high], hi2.at[m, h], ss.at[1], rs.at[1], dev(3)),
-            remote(src.at[up, high], hid.at[m, h], ss.at[2], rs.at[2], dev(1)),
-            remote(src.at[down, low], lod.at[m, h], ss.at[3], rs.at[3], dev(3)),
+            remote(src.at[far, low], lo2.at[m, h], ss, rs.at[0], dev(1)),
+            remote(src.at[far, high], hi2.at[m, h], ss, rs.at[1], dev(3)),
+            remote(src.at[up, high], hid.at[m, h], ss, rs.at[2], dev(1)),
+            remote(src.at[down, low], lod.at[m, h], ss, rs.at[3], dev(3)),
         )
 
     def relay_copies(m, h):
         p, dev = firsts[h]
-        ss, rs = s1_send.at[m, h], s1_recv.at[m, h]
+        ss, rs = send_sem.at[m], s1_recv.at[m, h]
         return (
-            remote(lo2.at[m, h], los.at[m, h], ss.at[4], rs.at[4], dev(1)),
-            remote(hi2.at[m, h], his.at[m, h], ss.at[5], rs.at[5], dev(3)),
+            remote(lo2.at[m, h], los.at[m, h], ss, rs.at[4], dev(1)),
+            remote(hi2.at[m, h], his.at[m, h], ss, rs.at[5], dev(3)),
         )
 
     def second_copies(m, h):
@@ -166,7 +187,7 @@
             remote(
                 piece.at[m, h, (p + k) % 4],
                 piece_in.at[m, h, k - 1],
-                s2_send.at[m, h, k - 1],
+                send_sem.at[m],
                 s2_recv.at[m, h, k - 1],
                 dev(k),
             )
@@ -179,7 +200,7 @@
             remote(
                 heads.at[m, h, slot_of(p, k)],
                 heads.at[m, h, slot_of(p, k)],
-                g1_send.at[m, h, k - 1],
+                send_sem.at[m],
                 g1_recv.at[m, h, k - 1],
                 dev(k),
             )
@@ -192,7 +213,7 @@
             remote(
                 lhs_in.at[m, h, slot_of(p, k)],
                 lhs_in.at[m, h, slot_of(p, k)],
-                g2_send.at[m, h, k - 1],
+                send_sem.at[m],
                 g2_recv.at[m, h, k - 1],
                 dev(k),
             )
@@ -210,7 +231,7 @@
             remote(
                 share.at[m, (gy + k) % 4],
                 share_in.at[m, k - 1],
-                gy_send.at[m, k - 1],
+                send_sem.at[m],
                 gy_recv.at[m, k - 1],
                 along_gy(k),
             )
@@ -219,12 +240,12 @@
 
     def x_copy_out(m, k):
         return remote(
-            result.at[m], xs.at[m, gy], x_send.at[m, k], x_recv.at[m, k], (1, gx, (gy + k) % 4)
+            result.at[m], xs.at[m, gy], x_send.at[m], x_recv.at[m, k], (1, gx, (gy + k) % 4)
         )
 
     def x_copy_in(m, k):
         slot = xs.at[m, (gy + 4 - k) % 4]
-        return remote(slot, slot, x_send.at[m, k], x_recv.at[m, k], (0, gx, gy))
+        return remote(slot, slot, x_send.at[m], x_recv.at[m, k], (0, gx, gy))
 
     def project(m):
         @pl.when((m == 0) & (sec == 0))
@@ -315,43 +336,52 @@
             k_copy.wait()
             v_copy.wait()
 
+        for h in range(2):
+            for copy in second_copies(m, h):
+                copy.wait_recv()
         inv_scale = 1.0 / 128**0.5
         slot = lax.broadcasted_iota(jnp.int32, (16, 1024), 1)
+        pairs = [(h, i) for h in range(2) for i in range(2)]
         for h in range(2):
             p, _ = seconds[h]
-            for copy in second_copies(m, h):
-                copy.wait_recv()
-            total[...] = piece[m, h, p] + piece_in[m, h, 0] + piece_in[m, h, 1] + piece_in[m, h, 2]
-            for s in range(2):
-                squares = jnp.sum(total[36 + s : 37 + s, :], axis=1, keepdims=True)
-                factor = lax.rsqrt(squares / MODEL_WIDTH + NORM_EPS)
-                cosine, sine = rope_ref[m, s, 0:1, :], rope_ref[m, s, 1:2, :]
-                query = total[16 * s : 16 * s + 16, :] * factor
-                query = (query * cosine + pltpu.roll(query, 64, 1) * sine).astype(jnp.bfloat16)
-                fresh_key = total[32 + s : 33 + s, :] * factor
-                fresh_key = fresh_key * cosine + pltpu.roll(fresh_key, 64, 1) * sine
-                fresh_key = fresh_key.astype(jnp.bfloat16).astype(jnp.float32)
-                fresh_value = (total[34 + s : 35 + s, :] * factor).astype(jnp.bfloat16).astype(jnp.float32)
-                scores = (
-                    lax.dot_general(
-                        query,
-                        keys[m, s, h],
-                        (((1,), (1,)), ((), ())),
-                        preferred_element_type=jnp.float32,
-                    )
-                    * inv_scale
+            total[h] = piece[m, h, p] + piece_in[m, h, 0] + piece_in[m, h, 1] + piece_in[m, h, 2]
+        queries, fresh_values, selves, scores = [], [], [], []
+        for h, i in pairs:
+            squares = jnp.sum(total[h, 36 + i : 37 + i, :], axis=1, keepdims=True)
+            factor = lax.rsqrt(squares / MODEL_WIDTH + NORM_EPS)
+            cosine, sine = rope_ref[0, pl.ds(2 * m + i, 1), :], rope_ref[1, pl.ds(2 * m + i, 1), :]
+            query = total[h, 16 * i : 16 * i + 16, :] * factor
+            query = (query * cosine + pltpu.roll(query, 64, 1) * sine).astype(jnp.bfloat16)
+            fresh_key = total[h, 32 + i : 33 + i, :] * factor
+            fresh_key = fresh_key * cosine + pltpu.roll(fresh_key, 64, 1) * sine
+            fresh_key = fresh_key.astype(jnp.bfloat16).astype(jnp.float32)
+            fresh_value = total[h, 34 + i : 35 + i, :] * factor
+            fresh_values.append(fresh_value.astype(jnp.bfloat16).astype(jnp.float32))
+            selves.append(jnp.sum(query.astype(jnp.float32) * fresh_key, axis=1, keepdims=True) * inv_scale)
+            queries.append(query)
+        for (h, i), query in zip(pairs, queries):
+            scores.append(
+                lax.dot_general(
+                    query, keys[m, i, h], (((1,), (1,)), ((), ())), preferred_element_type=jnp.float32
                 )
-                own = jnp.sum(query.astype(jnp.float32) * fresh_key, axis=1, keepdims=True) * inv_scale
-                scores = jnp.where(slot < len_ref[m, s], scores, -jnp.inf)
-                top = jnp.maximum(jnp.max(scores, axis=1, keepdims=True), own)
-                weights = jnp.exp(scores - top)
-                own = jnp.exp(own - top)
-                scale = 1.0 / (jnp.sum(weights, axis=1, keepdims=True) + own)
-                weights = (weights * scale).astype(jnp.bfloat16)
-                own = (own * scale).astype(jnp.bfloat16).astype(jnp.float32)
-                mixed = jnp.dot(weights, values[m, s, h], preferred_element_type=jnp.float32)
-                mixed = mixed + own * fresh_value
-                heads[m, h, p, 16 * s : 16 * s + 16, :] = mixed.astype(jnp.bfloat16)
+            )
+        weights, owns = [], []
+        for (h, i), score, own in zip(pairs, scores, selves):
+            score = jnp.where(slot < len_ref[i, m], score * inv_scale, -jnp.inf)
+            top = jnp.maximum(jnp.max(score, axis=1, keepdims=True), own)
+            weight = jnp.exp(score - top)
+            own = jnp.exp(own - top)
+            scale = 1.0 / (jnp.sum(weight, axis=1, keepdims=True) + own)
+            weights.append((weight * scale).astype(jnp.bfloat16))
+            owns.append((own * scale).astype(jnp.bfloat16).astype(jnp.float32))
+        mixes = [
+            jnp.dot(weight, values[m, i, h], preferred_element_type=jnp.float32)
+            for (h, i), weight in zip(pairs, weights)
+        ]
+        for (h, i), mixed, own, fresh_value in zip(pairs, mixes, owns, fresh_values):
+            p, _ = seconds[h]
+            heads[m, h, p, 16 * i : 16 * i + 16, :] = (mixed + own * fresh_value).astype(jnp.bfloat16)
+        for h in range(2):
             for copy in gather1_copies(m, h, sender_slot):
                 copy.start()
 
@@ -397,11 +427,11 @@
             copy.wait_recv()
         branch = share[m, gy] + share_in[m, 0] + share_in[m, 1] + share_in[m, 2]
         state = (xs[m, gy].astype(jnp.float32) + branch).astype(jnp.bfloat16)
-        out_ref[m] = state
+        result[m] = state
+        pltpu.make_async_copy(result.at[m], out_hbm.at[m], out_sem.at[m]).start()
 
         @pl.when(sec == 0)
         def _():
-            result[m] = state
             for k in range(4):
                 x_copy_out(m, k).start()
 
@@ -418,46 +448,36 @@
     lax.fori_loop(0, MICRO + STAGES - 1, moment, 0)
 
     def settle(m, carry):
-        for h in range(2):
-            for copy in (
-                *first_copies(m, h),
-                *relay_copies(m, h),
-                *second_copies(m, h),
-                *gather1_copies(m, h, sender_slot),
-                *gather2_copies(m, h, sender_slot),
-            ):
-                copy.wait_send()
-        for copy in gy_copies(m):
-            copy.wait_send()
+        remote(sent, sent, send_sem.at[m], out_sem.at[m], along_gy(1)).wait_send()
 
         @pl.when(sec == 0)
         def _():
-            for k in range(4):
-                x_copy_out(m, k).wait_send()
-
+            remote(xs.at[m], xs.at[m], x_send.at[m], out_sem.at[m], along_gy(1)).wait_send()
+
+        pltpu.make_async_copy(result.at[m], out_hbm.at[m], out_sem.at[m]).wait()
         return carry
 
     lax.fori_loop(0, MICRO, settle, 0)
 
 
 def body(inputs, gains, query_weight, key_value_weight, output_weight, key_cache, value_cache, lengths):
-    half = 64
-    frequency = ROPE_THETA ** (-2.0 * jnp.arange(half, dtype=jnp.float32) / 128)
-    angles = lengths.astype(jnp.float32)[:, :, None] * frequency
-    cosine, sine = jnp.cos(angles), jnp.sin(angles)
-    rope = jnp.stack(
-        [jnp.concatenate([cosine, cosine], axis=-1), jnp.concatenate([-sine, sine], axis=-1)], axis=2
-    )
+    frequency = (ROPE_THETA ** (-2.0 * (np.arange(128) % 64) / 128)).astype(np.float32)[None]
     f32, bf16 = jnp.float32, jnp.bfloat16
-    vmem, anywhere = pl.BlockSpec(memory_space=pltpu.VMEM), pl.BlockSpec(memory_space=pl.ANY)
+    anywhere = pl.BlockSpec(memory_space=pl.ANY)
     dma = pltpu.SemaphoreType.DMA
     low, high = pltpu.VMEM((4, 2, LOW, 128), f32), pltpu.VMEM((4, 2, HIGH, 128), f32)
     states = pl.pallas_call(
         kernel,
         out_shape=jax.ShapeDtypeStruct((MICRO, ROWS, 128), bf16),
-        in_specs=[anywhere, vmem, vmem, pl.BlockSpec(memory_space=pltpu.SMEM)] + [anywhere] * 5,
-        out_specs=vmem,
+        in_specs=[anywhere] * 9,
+        out_specs=anywhere,
         scratch_shapes=[
+            pltpu.VMEM((1, 512), bf16),
+            pltpu.VMEM((1, 128), f32),
+            pltpu.SMEM((2, MICRO), jnp.int32),
+            pltpu.VMEM((1, 512), f32),
+            pltpu.VMEM((2, 8, 128), f32),
+            pltpu.VMEM((SENT_ROWS, 128), f32),
             pltpu.VMEM((4, 4, ROWS, 128), bf16),
             pltpu.VMEM((2, 512, 2048), bf16),
             pltpu.VMEM((2, 512, 256), bf16),
@@ -476,7 +496,7 @@
             pltpu.VMEM((8 * TILES, 128), f32),
             pltpu.VMEM((4, 2, 4, 40, 128), f32),
             pltpu.VMEM((4, 2, 3, 40, 128), f32),
-            pltpu.VMEM((40, 128), f32),
+            pltpu.VMEM((2, 40, 128), f32),
             pltpu.VMEM((4, 2, 4, 32, 128), bf16),
             pltpu.VMEM((128, 128), f32),
             pltpu.VMEM((4, 2, 4, 16, 8, 128), bf16),
@@ -487,18 +507,15 @@
             pltpu.VMEM((4, 4, ROWS, 128), f32),
             pltpu.VMEM((4, 3, ROWS, 128), f32),
             pltpu.VMEM((4, ROWS, 128), bf16),
-            dma((11,)),
-            dma((4, 2, 6)),
+            dma((14,)),
+            dma((4,)),
+            dma((4,)),
             dma((4, 2, 6)),
             dma((4, 2, 3)),
             dma((4, 2, 3)),
             dma((4, 2, 3)),
-            dma((4, 2, 3)),
-            dma((4, 2, 3)),
-            dma((4, 2, 3)),
             dma((4, 3)),
-            dma((4, 3)),
-            dma((4, 4)),
+            dma((4,)),
             dma((4, 4)),
         ],
         compiler_params=pltpu.CompilerParams(
@@ -507,9 +524,9 @@
         name="relay_layers",
     )(
         inputs,
-        gains.astype(f32),
-        rope,
-        lengths,
+        gains,
+        jnp.asarray(frequency),
+        lengths.T,
         query_weight,
         key_value_weight,
         output_weight,

time: 83.9 us -> 74.7 us (0.89)
  Pallas kernels: 78 us -> 73.1 us
  other arithmetic: 2.78 us -> 0 us
  local copies, waits for them, and re-layouts: 2.8 us -> 1.38 us
    pallas_call x1, Pallas kernels: 78 us -> 73.1 us  [body(): pl.pallas_call(kernel, out_shape=jax.ShapeDtypeStruct((MICRO, ROWS, 128),...]
    convert_element_type x2 -> x0, other arithmetic: 1.93 us -> none  [the longest x1 1.25 us: body(): gains.astype(f32)]
    unnamed x2 -> x1, local copies, waits for them, and re-layouts: 2.71 us -> 1.38 us
where the time goes in v2:
time: 74.7 us; the launch traced here: 74.5 us
  Pallas kernels  73.1 us (98%)
  local copies, waits for them, and re-layouts  1.38 us (2%)
    pallas_call x1, Pallas kernels, body(): pl.pallas_call(kernel, out_shape=jax.ShapeDtypeStruct((MICRO, ROWS, 128),...  73.1 us

profile of v2, /device:TPU:5, one launch (start us, length us, event | category | flops | bytes accessed | tf_op | source)
XLA Modules:
  0.0 74.5 jit_solution(8037057474195371012)
XLA Ops:
  0.0 73.1 %relay_layers.1 = bf16[4,32,128]{2,1,0:T(8,128)(2,1)} custom-call(bf16[4,32,512]{2,1,0:T(8,128)(2,1)} %x_hbm.1, bf16[1,512]{1,0:T(2,128)(2,1)} %gain_hbm.1, f32[1,128]{1,0:T(1,128)} %constant.2.clone.freq_hbm, s32[2,4]{1,0:T(2,128)} %bitcast.3, bf16[1,512,4096]{2,1,0:T(8,128)(2,1)} %wq_hbm.1, bf16[1,512,512]{2,1,0:T(8,128)(2,1)} %wkv_hbm.1, ...), custom_call_target="tpu_custom_call" | custom-call | tf_op jit(solution)/shard_map/relay_layers/pallas_call | solution.py:469
  73.1 1.4 %copy.11 = bf16[1,4,32,128]{3,2,1,0:T(8,128)(2,1)} copy(bf16[1,4,32,128]{3,2,1,0:T(8,128)(2,1)} %bitcast.2) | data formatting | bytes 65536

commit v3 on v2

--- a/solution.py
+++ b/solution.py
@@ -14,8 +14,9 @@
 MICRO = 4
 ROWS = 32
 TILES = 19
-LOW = 80
-HIGH = 72
+LOW_TILES = 10
+LOW = 8 * LOW_TILES
+HIGH = 8 * (TILES - LOW_TILES)
 STAGES = 7
 SENT_ROWS = 1728
 
@@ -75,6 +76,7 @@
     local_sem,
     send_sem,
     out_sem,
+    ready_sem,
     s1_recv,
     s2_recv,
     g1_recv,
@@ -106,6 +108,18 @@
             src_ref=src, dst_ref=dst, send_sem=send, recv_sem=recv, device_id=dev, device_id_type=MESH
         )
 
+    barrier = pltpu.get_barrier_semaphore()
+    partners = [along(k) for along in (along_z, along_y, along_gy) for k in (1, 2, 3)]
+    for dev in partners:
+        pl.semaphore_signal(barrier, inc=1, device_id=dev, device_id_type=MESH)
+
+    @pl.when(sec == 0)
+    def _():
+        for k in range(4):
+            pl.semaphore_signal(
+                barrier, inc=1, device_id=(1, gx, (gy + k) % 4), device_id_type=MESH
+            )
+
     local = []
 
     def stage_in(src, dst):
@@ -113,19 +127,26 @@
         local.append(copy)
         return copy
 
-    small = [stage_in(gain_hbm, gain_in), stage_in(freq_hbm, freq_in), stage_in(len_hbm, len_ref)]
+    gain_copy = stage_in(gain_hbm, gain_in)
+    rope_copies = [stage_in(freq_hbm, freq_in), stage_in(len_hbm, len_ref)]
     x_copies = [stage_in(x_hbm.at[:, :, pl.ds(128 * c, 128)], xs.at[:, c]) for c in range(4)]
-    wq_copies = []
-    wkv_copies = []
+    low_copies, high_copies = [], []
     for h in range(2):
-        wq_copies.append(stage_in(wq_hbm.at[0, :, pl.ds(2048 * h, 2048)], wq.at[h]))
-        wkv_copies.append(stage_in(wkv_hbm.at[0, :, pl.ds(256 * h, 256)], wkv.at[h]))
+        cut = 128 * LOW_TILES
+        low_copies.append(stage_in(wq_hbm.at[0, :, pl.ds(2048 * h, cut)], wq.at[h, :, pl.ds(0, cut)]))
+        high_copies.append(
+            (
+                stage_in(
+                    wq_hbm.at[0, :, pl.ds(2048 * h + cut, 2048 - cut)], wq.at[h, :, pl.ds(cut, 2048 - cut)]
+                ),
+                stage_in(wkv_hbm.at[0, :, pl.ds(256 * h, 256)], wkv.at[h]),
+            )
+        )
     k_copy = stage_in(k_hbm.at[0], keys)
     v_copy = stage_in(v_hbm.at[0], values)
     wo_copy = stage_in(wo_hbm.at[0], wo)
 
-    for copy in small:
-        copy.start()
+    gain_copy.start()
 
     @pl.when(sec == 0)
     def _():
@@ -133,32 +154,39 @@
             copy.start()
 
     for h in range(2):
-        wq_copies[h].start()
-        wkv_copies[h].start()
+        low_copies[h].start()
+        for copy in high_copies[h]:
+            copy.start()
+    for copy in rope_copies:
+        copy.start()
     k_copy.start()
     v_copy.start()
     wo_copy.start()
 
-    barrier = pltpu.get_barrier_semaphore()
-    partners = [along_z(k) for k in (1, 2, 3)] + [along_y(k) for k in (1, 2, 3)]
-    partners += [along_gy(k) for k in (1, 2, 3)]
-    partners += [(1 - sec, gx, (gy + k) % 4) for k in range(4)]
-    for dev in partners:
-        pl.semaphore_signal(barrier, inc=1, device_id=dev, device_id_type=MESH)
-
-    for copy in small:
-        copy.wait()
+    @pl.when(sec == 1)
+    def _():
+        pl.semaphore_wait(barrier, len(partners) + 4)
+        for k in range(4):
+            pl.semaphore_signal(
+                ready_sem, inc=1, device_id=(0, gx, (gy + k) % 4), device_id_type=MESH
+            )
+
+    gain_copy.wait()
     gain_ref[...] = gain_in[...].astype(jnp.float32)
-    row = lax.broadcasted_iota(jnp.int32, (8, 128), 0)
-    lane = lax.broadcasted_iota(jnp.int32, (8, 128), 1)
-    spots = jnp.zeros((8, 128), jnp.int32)
-    for m in range(MICRO):
-        for i in range(2):
-            spots = jnp.where(row == 2 * m + i, len_ref[i, m], spots)
-    angles = spots.astype(jnp.float32) * freq_in[...]
-    sine = jnp.sin(angles)
-    rope_ref[0] = jnp.cos(angles)
-    rope_ref[1] = jnp.where(lane < 64, -sine, sine)
+
+    def make_rope():
+        for copy in rope_copies:
+            copy.wait()
+        row = lax.broadcasted_iota(jnp.int32, (8, 128), 0)
+        lane = lax.broadcasted_iota(jnp.int32, (8, 128), 1)
+        spots = jnp.zeros((8, 128), jnp.int32)
+        for m in range(MICRO):
+            for i in range(2):
+                spots = jnp.where(row == 2 * m + i, len_ref[i, m], spots)
+        angles = spots.astype(jnp.float32) * freq_in[...]
+        sine = jnp.sin(angles)
+        rope_ref[0] = jnp.cos(angles)
+        rope_ref[1] = jnp.where(lane < 64, -sine, sine)
 
     def first_copies(m, h):
         p, dev = firsts[h]
@@ -226,17 +254,16 @@
     def receiver_slot(p, k):
         return (p + 4 - k) % 4
 
-    def gy_copies(m):
-        return [
-            remote(
-                share.at[m, (gy + k) % 4],
-                share_in.at[m, k - 1],
-                send_sem.at[m],
-                gy_recv.at[m, k - 1],
-                along_gy(k),
-            )
-            for k in (1, 2, 3)
-        ]
+    def gy_copy(m, k, far):
+        peer = (2 * (1 - gy // 2) + k - 2) if far else 4 * (gy // 2) + 1 - gy
+        slot = (1 + gy % 2) if far else 0
+        return remote(
+            share.at[m, peer], share_in.at[m, slot], send_sem.at[m], gy_recv.at[m, slot], (sec, gx, peer)
+        )
+
+    def gy_arrival(m, slot):
+        ref = share_in.at[m, slot]
+        return remote(ref, ref, send_sem.at[m], gy_recv.at[m, slot], along_gy(1))
 
     def x_copy_out(m, k):
         return remote(
@@ -247,11 +274,13 @@
         slot = xs.at[m, (gy + 4 - k) % 4]
         return remote(slot, slot, x_send.at[m], x_recv.at[m, k], (0, gx, gy))
 
-    def project(m):
-        @pl.when((m == 0) & (sec == 0))
-        def _():
-            for copy in x_copies:
-                copy.wait()
+    def project(m, opening=False):
+        if opening:
+
+            @pl.when(sec == 0)
+            def _():
+                for copy in x_copies:
+                    copy.wait()
 
         @pl.when(sec == 1)
         def _():
@@ -261,12 +290,6 @@
         for c in range(4):
             wide[c] = xs[m, c].astype(jnp.float32)
         for h in range(2):
-
-            @pl.when(m == 0)
-            def _(h=h):
-                wq_copies[h].wait()
-                wkv_copies[h].wait()
-
             if h == 1:
                 for c in range(4):
                     swapped_rows(wide.at[c], turned.at[c])
@@ -275,27 +298,43 @@
                 [(b * gain_ref[:, 128 * c : 128 * c + 128]).astype(jnp.bfloat16) for c, b in enumerate(blocks)],
                 axis=1,
             )
+
+            def multiply(weight, tile, h=h, scaled=scaled):
+                sums = jnp.dot(scaled, weight, preferred_element_type=jnp.float32)
+                for c in range(4):
+                    for j in range(weight.shape[1] // 128):
+                        part[m, h, c, 8 * (tile + j) : 8 * (tile + j) + 8, :] = sums[
+                            8 * c : 8 * c + 8, 128 * j : 128 * j + 128
+                        ]
+
             squares = sum(b * b for b in blocks[1:]) + blocks[0] * blocks[0]
             for c in range(4):
                 part[m, h, c, 144:152, :] = squares[8 * c : 8 * c + 8, :]
-            for col in range(5):
-                width = 512 if col < 4 else 256
-                weight = wq[h, :, 512 * col : 512 * col + 512] if col < 4 else wkv[h]
-                sums = jnp.dot(scaled, weight, preferred_element_type=jnp.float32)
-                for c in range(4):
-                    for j in range(width // 128):
-                        tile = 4 * col + j
-                        part[m, h, c, 8 * tile : 8 * tile + 8, :] = sums[
-                            8 * c : 8 * c + 8, 128 * j : 128 * j + 128
-                        ]
-            if h == 0:
-
-                @pl.when(m == 0)
-                def _():
-                    pl.semaphore_wait(barrier, len(partners))
-
-            for copy in first_copies(m, h):
-                copy.start()
+            lo_up, hi_down, hi_up, lo_down = first_copies(m, h)
+            if opening:
+                low_copies[h].wait()
+                multiply(wq[h, :, 0:768], 0)
+                multiply(wq[h, :, 768 : 128 * LOW_TILES], 6)
+                if h == 0:
+
+                    @pl.when(sec == 0)
+                    def _():
+                        pl.semaphore_wait(barrier, len(partners))
+
+                lo_up.start()
+                lo_down.start()
+                for copy in high_copies[h]:
+                    copy.wait()
+                multiply(wq[h, :, 128 * LOW_TILES : 2048], LOW_TILES)
+                multiply(wkv[h], 16)
+            else:
+                for col in range(4):
+                    multiply(wq[h, :, 512 * col : 512 * col + 512], 4 * col)
+                multiply(wkv[h], 16)
+                lo_up.start()
+                lo_down.start()
+            hi_down.start()
+            hi_up.start()
 
     def relay(m):
         for h in range(2):
@@ -407,45 +446,52 @@
                 copy.wait_recv()
             for j in range(16):
                 rows = [lhs_in[m, h, b, j].astype(jnp.float32) for b in range(4)]
-                lhs[:, 128 * j : 128 * j + 128] = jnp.concatenate(rows, axis=0).astype(jnp.bfloat16)
-            sums = jnp.dot(
-                lhs[...], wo[2048 * h : 2048 * h + 2048, :], preferred_element_type=jnp.float32
-            )
-            if h == 0:
-                branch0[...] = sums
-            else:
-                branch1[...] = sums
-        swapped_rows(branch1, branch2)
-        for c in range(4):
-            cols = slice(128 * c, 128 * c + 128)
-            share[m, c] = branch0[:, cols] + branch2[:, cols]
-        for copy in gy_copies(m):
-            copy.start()
+                lhs[h, :, 128 * j : 128 * j + 128] = jnp.concatenate(rows, axis=0).astype(jnp.bfloat16)
+        near = gy // 2
+        for side in (1 - near, near):
+            cols = pl.ds(pl.multiple_of(256 * side, 256), 256)
+            branch0[...] = jnp.dot(lhs[0], wo[0:2048, cols], preferred_element_type=jnp.float32)
+            branch1[...] = jnp.dot(lhs[1], wo[2048:4096, cols], preferred_element_type=jnp.float32)
+            swapped_rows(branch1, branch2)
+            for c in range(2):
+                share[m, 2 * side + c] = (
+                    branch0[:, 128 * c : 128 * c + 128] + branch2[:, 128 * c : 128 * c + 128]
+                )
+            if side is not near:
+                for k in (2, 3):
+                    gy_copy(m, k, far=True).start()
+        gy_copy(m, 1, far=False).start()
 
     def finish(m):
-        for copy in gy_copies(m):
-            copy.wait_recv()
+        for slot in range(3):
+            gy_arrival(m, slot).wait_recv()
         branch = share[m, gy] + share_in[m, 0] + share_in[m, 1] + share_in[m, 2]
         state = (xs[m, gy].astype(jnp.float32) + branch).astype(jnp.bfloat16)
         result[m] = state
         pltpu.make_async_copy(result.at[m], out_hbm.at[m], out_sem.at[m]).start()
 
+        @pl.when((sec == 0) & (m == 0))
+        def _():
+            pl.semaphore_wait(ready_sem, 4)
+
         @pl.when(sec == 0)
         def _():
             for k in range(4):
                 x_copy_out(m, k).start()
 
     def moment(t, carry):
-        for n, stage in enumerate((project, relay, second, attend, regroup, output, finish)):
+        for n, stage in ((0, project), (2, relay), (4, second), (6, attend), (8, regroup), (10, output), (12, finish)):
             m = t - n
 
-            @pl.when((m >= 0) & (m < MICRO))
+            @pl.when((m >= (1 if n == 0 else 0)) & (m < MICRO))
             def _(stage=stage, m=m):
                 stage(m)
 
         return carry
 
-    lax.fori_loop(0, MICRO + STAGES - 1, moment, 0)
+    project(0, opening=True)
+    make_rope()
+    lax.fori_loop(1, MICRO + 12, moment, 0)
 
     def settle(m, carry):
         remote(sent, sent, send_sem.at[m], out_sem.at[m], along_gy(1)).wait_send()
@@ -500,16 +546,17 @@
             pltpu.VMEM((4, 2, 4, 32, 128), bf16),
             pltpu.VMEM((128, 128), f32),
             pltpu.VMEM((4, 2, 4, 16, 8, 128), bf16),
-            pltpu.VMEM((ROWS, 2048), bf16),
-            pltpu.VMEM((ROWS, 512), f32),
-            pltpu.VMEM((ROWS, 512), f32),
-            pltpu.VMEM((ROWS, 512), f32),
+            pltpu.VMEM((2, ROWS, 2048), bf16),
+            pltpu.VMEM((ROWS, 256), f32),
+            pltpu.VMEM((ROWS, 256), f32),
+            pltpu.VMEM((ROWS, 256), f32),
             pltpu.VMEM((4, 4, ROWS, 128), f32),
             pltpu.VMEM((4, 3, ROWS, 128), f32),
             pltpu.VMEM((4, ROWS, 128), bf16),
-            dma((14,)),
+            dma((16,)),
             dma((4,)),
             dma((4,)),
+            pltpu.SemaphoreType.REGULAR,
             dma((4, 2, 6)),
             dma((4, 2, 3)),
             dma((4, 2, 3)),

time: 74.7 us -> 71.8 us (0.961)
  Pallas kernels: 73.1 us -> 70.3 us
    pallas_call x1, Pallas kernels: 73.1 us -> 70.3 us  [body(): pl.pallas_call(kernel, out_shape=jax.ShapeDtypeStruct((MICRO, ROWS, 128),...]
where the time goes in v3:
time: 71.8 us; the launch traced here: 71.7 us
  Pallas kernels  70.3 us (98%)
  local copies, waits for them, and re-layouts  1.38 us (2%)
    pallas_call x1, Pallas kernels, body(): pl.pallas_call(kernel, out_shape=jax.ShapeDtypeStruct((MICRO, ROWS, 128),...  70.3 us

profile of v3, /device:TPU:5, one launch (start us, length us, event | category | flops | bytes accessed | tf_op | source)
XLA Modules:
  0.0 71.7 jit_solution(8983695368138713770)
XLA Ops:
  0.0 70.3 %relay_layers.1 = bf16[4,32,128]{2,1,0:T(8,128)(2,1)} custom-call(bf16[4,32,512]{2,1,0:T(8,128)(2,1)} %x_hbm.1, bf16[1,512]{1,0:T(2,128)(2,1)} %gain_hbm.1, f32[1,128]{1,0:T(1,128)} %constant.2.clone.freq_hbm, s32[2,4]{1,0:T(2,128)} %bitcast.3, bf16[1,512,4096]{2,1,0:T(8,128)(2,1)} %wq_hbm.1, bf16[1,512,512]{2,1,0:T(8,128)(2,1)} %wkv_hbm.1, ...), custom_call_target="tpu_custom_call" | custom-call | tf_op jit(solution)/shard_map/relay_layers/pallas_call | solution.py:515
  70.3 1.4 %copy.11 = bf16[1,4,32,128]{3,2,1,0:T(8,128)(2,1)} copy(bf16[1,4,32,128]{3,2,1,0:T(8,128)(2,1)} %bitcast.2) | data formatting | bytes 65536
